TPU v7x, 32 devices: a whole 2x2x4 slice. The times are simulated.
32 devices in a mesh: dp: 4 (over y, x), centers: 8 (over z, core).
Axes of the slice: x: 2, y: 2, z: 4, core: 2. Of those that a mesh axis runs over, the one named last changes fastest.
Arguments:
- points: bfloat16 [16384, 32], P('dp'), may hold values from -6 to 6
- centers: bfloat16 [16384, 32], P('centers'), may hold values from -6 to 6
- coef: bfloat16 [16384, 64], P('centers'), may hold values from -0.1875 to 0.1875
Outputs:
- product: float32 [16384, 64], P('centers')
All inputs are finite; a program needn't handle non-finite values.
Results may differ from a plain program's by a relative error of at most 0.0003.
Values may be sent and summed in bfloat16 or wider, within the bound.
A program may use at most 128 MiB of HBM per device.

v0:
```python
import jax
import jax.numpy as jnp
from jax import lax
from jax.sharding import PartitionSpec as P


def kernel_block(left_pts, left_sq, right_pts, right_sq, features):
    inner = lax.dot_general(
        left_pts, right_pts, (((1,), (1,)), ((), ())), preferred_element_type=jnp.float32
    )
    dist = left_sq[:, None] + right_sq[None, :] - 2.0 * inner
    return jnp.exp(dist * (-2.0 / features)).astype(jnp.bfloat16)


def squares(values):
    wide = values.astype(jnp.float32)
    return jnp.sum(wide * wide, axis=1)


def on_device(points, centers, coef):
    features = points.shape[1]
    local_pts = points.shape[0]
    local_cen = centers.shape[0]
    outs_count = coef.shape[1]
    block_pts = min(1024, local_pts)
    block_count = local_pts // block_pts
    cen_sq = squares(centers)
    point_blocks = points.reshape(block_count, block_pts, features)
    scalar_zero = jnp.zeros((), jnp.float32)

    def forward_keep(carry, block):
        kernel = kernel_block(block, squares(block), centers, cen_sq, features)
        return (carry, (kernel, jnp.dot(kernel, coef, preferred_element_type=jnp.float32)))

    unused, (tiles, partial_value) = lax.scan(forward_keep, scalar_zero, point_blocks)
    forward_part = partial_value.reshape(local_pts, outs_count)
    shared = lax.psum_scatter(
        forward_part.astype(jnp.bfloat16), "centers", scatter_dimension=0, tiled=True
    )
    forward = lax.all_gather(shared, "centers", axis=0, tiled=True)
    forward_blocks = forward.reshape(block_count, block_pts, outs_count)
    back = jnp.einsum("bij,bio->jo", tiles, forward_blocks, preferred_element_type=jnp.float32)
    total_pts = local_pts * lax.axis_size("dp")
    back = back * (1.0 / jnp.sqrt(jnp.float32(total_pts)))
    own_count = local_cen // lax.axis_size("dp")
    own_start = lax.axis_index("dp") * own_count
    own_cen = lax.dynamic_slice_in_dim(centers, own_start, own_count, 0)
    own_sq = squares(own_cen)
    piece_cen = lax.all_gather(centers, "centers", axis=0, tiled=True)
    piece_coef = lax.all_gather(coef, "centers", axis=0, tiled=True)
    kernel = kernel_block(own_cen, own_sq, piece_cen, squares(piece_cen), features)
    regular = jnp.dot(kernel, piece_coef, preferred_element_type=jnp.float32)
    placed = lax.dynamic_update_slice_in_dim(jnp.zeros_like(back), regular, own_start, 0)
    return lax.psum(back + placed, "dp")


def solution(mesh):
    in_specs = (P("dp", None), P("centers", None), P("centers", None))
    out_specs = P("centers", None)
    return jax.shard_map(
        on_device, mesh=mesh, in_specs=in_specs, out_specs=out_specs, check_vma=False
    )
```

profile of v0, /device:TPU:0, one launch (start us, length us, event | category | flops | bytes accessed | tf_op | source)
XLA Modules:
  0.0 192.9 jit_solution(11572367523075643524)
XLA Ops:
  6.5 1.4 copy.5
  8.0 1.0 multiply_reduce_fusion.2
  8.9 27.9 %while.12 = (s32[]{:T(128)}, bf16[4,1024,2048]{2,1,0:T(8,128)(2,1)}, bf16[4,1024,64]{1,2,0:T(8,128)(2,1)S(1)}, bf16[4,1024,32]{2,1,0:T(8,128)(2,1)S(1)}, f32[204...) while((s32[]{:T(128)}, bf16[4,1024,2048]{2,1,0:T(8,128)(2,1)}, ...), condition=%wide.region_3.4_spmd, body=%wide.region_1.3_spmd.sunk | while | flops 413236224 | bytes 13583461 | solution.py:35
  9.2 4.4 %bitcast_dynamic-update-slice_fusion.2 = (bf16[4,1024,2048]{2,1,0:T(8,128)(2,1)}, bf16[1024,2048]{1,0:T(8,128)(2,1)S(1)}) fusion(bf16[4,1024,2048]{2,1,0:T(8,128)(2,1)} %get-tuple-element.117, s32[]{:T(128)S(6)} %copy.19, bf16[2048,32]{0,1:T(8,128)(2,1)} %get-tuple-element.129, bf16[4,1024,32]{2,1,0:T(8,128)(2,1)S(1)} %get-tuple-element.127, ...), kind=kOutput, calls=%fused_computation.1.clone.1 | convolution fusion | flops 144703488 | bytes 8795136 | tf_op jit(solution)/shard_map/while/body/eval_jaxpr/dot_general | solution.py:8
  13.5 2.3 %fusion.29 = bf16[4,1024,64]{1,2,0:T(8,128)(2,1)S(1)} fusion(bf16[4,1024,64]{1,2,0:T(8,128)(2,1)S(1)} %get-tuple-element.118, s32[]{:T(128)S(6)} %copy.19, bf16[1024,2048]{1,0:T(8,128)(2,1)S(1)} %get-tuple-element.107, bf16[2048,64]{0,1:T(8,128)(2,1)} %get-tuple-element.130), kind=kOutput, calls=%fused_computation.3.clone.1 | convolution fusion | flops 268435456 | bytes 4718596 | tf_op jit(solution)/shard_map/while/body/eval_jaxpr/dot_general | solution.py:33
  16.1 4.4 %bitcast_dynamic-update-slice_fusion.2 = (bf16[4,1024,2048]{2,1,0:T(8,128)(2,1)}, bf16[1024,2048]{1,0:T(8,128)(2,1)S(1)}) fusion(bf16[4,1024,2048]{2,1,0:T(8,128)(2,1)} %get-tuple-element.117, s32[]{:T(128)S(6)} %copy.19, bf16[2048,32]{0,1:T(8,128)(2,1)} %get-tuple-element.129, bf16[4,1024,32]{2,1,0:T(8,128)(2,1)S(1)} %get-tuple-element.127, ...), kind=kOutput, calls=%fused_computation.1.clone.1 | convolution fusion | flops 144703488 | bytes 8795136 | tf_op jit(solution)/shard_map/while/body/eval_jaxpr/dot_general | solution.py:8
  20.5 2.3 %fusion.29 = bf16[4,1024,64]{1,2,0:T(8,128)(2,1)S(1)} fusion(bf16[4,1024,64]{1,2,0:T(8,128)(2,1)S(1)} %get-tuple-element.118, s32[]{:T(128)S(6)} %copy.19, bf16[1024,2048]{1,0:T(8,128)(2,1)S(1)} %get-tuple-element.107, bf16[2048,64]{0,1:T(8,128)(2,1)} %get-tuple-element.130), kind=kOutput, calls=%fused_computation.3.clone.1 | convolution fusion | flops 268435456 | bytes 4718596 | tf_op jit(solution)/shard_map/while/body/eval_jaxpr/dot_general | solution.py:33
  23.1 4.4 %bitcast_dynamic-update-slice_fusion.2 = (bf16[4,1024,2048]{2,1,0:T(8,128)(2,1)}, bf16[1024,2048]{1,0:T(8,128)(2,1)S(1)}) fusion(bf16[4,1024,2048]{2,1,0:T(8,128)(2,1)} %get-tuple-element.117, s32[]{:T(128)S(6)} %copy.19, bf16[2048,32]{0,1:T(8,128)(2,1)} %get-tuple-element.129, bf16[4,1024,32]{2,1,0:T(8,128)(2,1)S(1)} %get-tuple-element.127, ...), kind=kOutput, calls=%fused_computation.1.clone.1 | convolution fusion | flops 144703488 | bytes 8795136 | tf_op jit(solution)/shard_map/while/body/eval_jaxpr/dot_general | solution.py:8
  27.5 2.3 %fusion.29 = bf16[4,1024,64]{1,2,0:T(8,128)(2,1)S(1)} fusion(bf16[4,1024,64]{1,2,0:T(8,128)(2,1)S(1)} %get-tuple-element.118, s32[]{:T(128)S(6)} %copy.19, bf16[1024,2048]{1,0:T(8,128)(2,1)S(1)} %get-tuple-element.107, bf16[2048,64]{0,1:T(8,128)(2,1)} %get-tuple-element.130), kind=kOutput, calls=%fused_computation.3.clone.1 | convolution fusion | flops 268435456 | bytes 4718596 | tf_op jit(solution)/shard_map/while/body/eval_jaxpr/dot_general | solution.py:33
  30.1 4.4 %bitcast_dynamic-update-slice_fusion.2 = (bf16[4,1024,2048]{2,1,0:T(8,128)(2,1)}, bf16[1024,2048]{1,0:T(8,128)(2,1)S(1)}) fusion(bf16[4,1024,2048]{2,1,0:T(8,128)(2,1)} %get-tuple-element.117, s32[]{:T(128)S(6)} %copy.19, bf16[2048,32]{0,1:T(8,128)(2,1)} %get-tuple-element.129, bf16[4,1024,32]{2,1,0:T(8,128)(2,1)S(1)} %get-tuple-element.127, ...), kind=kOutput, calls=%fused_computation.1.clone.1 | convolution fusion | flops 144703488 | bytes 8795136 | tf_op jit(solution)/shard_map/while/body/eval_jaxpr/dot_general | solution.py:8
  34.5 2.3 %fusion.29 = bf16[4,1024,64]{1,2,0:T(8,128)(2,1)S(1)} fusion(bf16[4,1024,64]{1,2,0:T(8,128)(2,1)S(1)} %get-tuple-element.118, s32[]{:T(128)S(6)} %copy.19, bf16[1024,2048]{1,0:T(8,128)(2,1)S(1)} %get-tuple-element.107, bf16[2048,64]{0,1:T(8,128)(2,1)} %get-tuple-element.130), kind=kOutput, calls=%fused_computation.3.clone.1 | convolution fusion | flops 268435456 | bytes 4718596 | tf_op jit(solution)/shard_map/while/body/eval_jaxpr/dot_general | solution.py:33
  36.8 0.8 copy.9
  37.7 0.7 all-gather.3.cloned.1.call-update
  38.5 0.7 all-gather.5.cloned.1.call-update
  39.2 0.8 multiply_reduce_fusion.3
  40.0 31.9 %reduce-scatter.2.cloned.1.call-done = bf16[512,64]{0,1:T(8,128)(2,1)} async-done(((bf16[4096,64]{0,1:T(8,128)(2,1)}), bf16[512,64]{0,1:T(8,128)(2,1)}) %reduce-scatter.2.cloned.1.call-update) | async-done | bytes 65552 | tf_op jit(solution)/shard_map/reduce_scatter | solution.py:37
  71.9 16.8 %all_gather.9 = bf16[4096,64]{0,1:T(8,128)(2,1)S(1)} all-gather(bf16[512,64]{0,1:T(8,128)(2,1)} %reduce-scatter.2.cloned.1.call-done), channel_id=1, replica_groups=mesh['dp'=4,'centers'=8] {'centers'}, dimensions={0}, use_global_device_ids=true | all-gather | bytes 589824 | tf_op jit(solution)/shard_map/all_gather | solution.py:40
  88.7 8.9 %fusion.5 = f32[2048,64]{0,1:T(8,128)S(1)} fusion(bf16[4,1024,2048]{2,1,0:T(8,128)(2,1)} %get-tuple-element.43, bf16[8,4,8,1024]{3,2,1,0:T(8,128)(2,1)S(1)} %bitcast.46), kind=kOutput, calls=%fused_computation.11 | convolution fusion | flops 1073872896 | bytes 17825792 | tf_op jit(solution)/shard_map/bij,bio->jo/dot_general | solution.py:42
  97.6 1.5 multiply_reduce_fusion.1
  99.2 26.4 %all-gather.5.cloned.1.call-done = bf16[16384,64]{0,1:T(8,128)(2,1)} async-done(((bf16[2048,64]{0,1:T(8,128)(2,1)}), bf16[16384,64]{0,1:T(8,128)(2,1)}) %all-gather.5.cloned.1.call-update) | async-done | bytes 2097168 | tf_op jit(solution)/shard_map/all_gather | solution.py:50
  125.6 13.2 %fusion.7 = f32[2048,64]{0,1:T(8,128)S(1)} fusion(f32[2048,64]{0,1:T(8,128)S(1)} %fusion.5, s32[]{:T(128)S(6)} %select_n.4, bf16[16384,64]{0,1:T(8,128)(2,1)} %all-gather.5.cloned.1.call-done, bf16[16384,32]{0,1:T(8,128)(2,1)} %all-gather.3.cloned.1.call-done, f32[16384]{0:T(1024)S(1)} %multiply_reduce_fusion.1, f32[512]{0:T(512)S(1)} %multiply_reduce_fusion.3, ...), kind=kOutput, calls=%fused_computation.14 | convolution fusion | flops 1652588544 | bytes 3509248 | tf_op jit(solution)/shard_map/dot_general | solution.py:52
  138.8 0.8 copy-done
  139.6 44.9 %all-reduce.2.cloned.1.call-done = f32[2048,64]{0,1:T(8,128)} async-done(((f32[2048,64]{0,1:T(8,128)}), f32[2048,64]{0,1:T(8,128)}) %all-reduce.2.cloned.1.call-update) | async-done | bytes 524304 | tf_op jit(solution)/shard_map/psum | solution.py:54
  184.5 1.9 copy.27
  (14 shorter events, 1.0 us)
Async XLA Ops:
  6.5 65.4 %reduce-scatter.2.cloned.1.call-start = ((), (), s32[]{:S(2)}) async-start(), calls=%async_computation.1 | async-start | bytes 589824 | tf_op jit(solution)/shard_map/reduce_scatter | solution.py:37
  37.7 59.9 %all-gather.3.cloned.1.call-start = ((), (), s32[]{:S(2)}) async-start(), calls=%async_computation.2 | async-start | bytes 1179648 | tf_op jit(solution)/shard_map/all_gather | solution.py:49
  38.4 87.2 %all-gather.5.cloned.1.call-start = ((), (), s32[]{:S(2)}) async-start(), calls=%async_computation.3 | async-start | bytes 2359296 | tf_op jit(solution)/shard_map/all_gather | solution.py:50
  39.2 145.4 %all-reduce.2.cloned.1.call-start = ((), (), s32[]{:S(2)}) async-start(), calls=%async_computation.4 | async-start | bytes 1048576 | tf_op jit(solution)/shard_map/psum | solution.py:54
  138.8 0.8 copy-start
Sparse Core Ops, SparseCore 0:
  37.8 34.0 reduce-scatter.1
  73.5 21.7 all-gather.2
  96.9 28.6 all-gather.4
  139.7 44.7 all-reduce.1
where the time goes:
time: 193 us
  waiting for transfers between devices  105 us (54%)
  matrix products  49 us (25%)
  blocking collectives  16.8 us (9%)
  between operations  13.2 us (7%)
  local copies, waits for them, and re-layouts  4.92 us (3%)
  other arithmetic  4.13 us (2%)
    psum x1, waiting for transfers between devices, on_device(): return lax.psum(back + placed, 'dp')  44.9 us
    reduce_scatter x1, waiting for transfers between devices, on_device(): lax.psum_scatter(forward_part.astype(jnp.bfloat16), 'centers', scatter_di...  31.9 us
    all_gather x1, waiting for transfers between devices, on_device(): piece_coef = lax.all_gather(coef, 'centers', axis=0, tiled=True)  26.4 us
    dot_general x4, matrix products, kernel_block(): lax.dot_general(left_pts, right_pts, (((1,), (1,)), ((), ())), preferred_...  17.6 us
    all_gather x1, blocking collectives, on_device(): forward = lax.all_gather(shared, 'centers', axis=0, tiled=True)  16.8 us
    dot_general x1, matrix products, on_device(): regular = jnp.dot(kernel, piece_coef, preferred_element_type=jnp.float32)  13.2 us
    dot_general x4, matrix products, forward_keep(): jnp.dot(kernel, coef, preferred_element_type=jnp.float32)  9.35 us
    dot_general x1, matrix products, on_device(): jnp.einsum('bij,bio->jo', tiles, forward_blocks, preferred_element_type=j...  8.89 us
  transfers between devices with their start and end apart: 4, of which 3 were waited for; matrix products, arithmetic and copies ran while one was open for 6% of the time, Pallas kernels for 0%

commit v1 on v0

v1 whole, which is shorter than its diff:
```python
import functools
import math

import jax
import jax.numpy as jnp
from jax import lax
from jax.experimental import pallas as pl
from jax.experimental.pallas import tpu as pltpu
from jax.sharding import PartitionSpec as P

MESH = pl.DeviceIdType.MESH
F32, BF16 = jnp.float32, jnp.bfloat16


def dot(a, b):
    return lax.dot_general(a, b, (((1,), (0,)), ((), ())), preferred_element_type=F32)


def dot_nt(a, b):
    return lax.dot_general(a, b, (((1,), (1,)), ((), ())), preferred_element_type=F32)


def split3(v):
    hi = v.astype(BF16).astype(F32)
    mid = (v - hi).astype(BF16).astype(F32)
    return hi, mid, (v - hi) - mid


def row_form(x, width):
    feats = x.shape[1]
    lane = lax.broadcasted_iota(jnp.int32, (feats, width), 1)
    sub = lax.broadcasted_iota(jnp.int32, (feats, width), 0)
    pick = ((lane % feats) == sub) & (lane < 3 * feats)
    spread = dot(x, pick.astype(F32).astype(BF16))
    wide = x.astype(F32)
    sq = jnp.sum(wide * wide, axis=1, keepdims=True) * (-2.0 * math.log2(math.e) / feats)
    hi, mid, lo = split3(sq)
    at = lax.broadcasted_iota(jnp.int32, (x.shape[0], width), 1) - 3 * feats
    tail = jnp.where(at == 3, hi, jnp.where(at == 4, mid, jnp.where(at == 5, lo, 0.0)))
    tail = jnp.where((at >= 0) & (at < 3), 1.0, tail)
    return (spread + tail).astype(BF16)


def col_form(ct, width):
    feats, count = ct.shape
    wide = ct.astype(F32)
    parts = [p.astype(BF16) for p in split3(wide * (4.0 * math.log2(math.e) / feats))]
    sq = jnp.sum(wide * wide, axis=0, keepdims=True) * (-2.0 * math.log2(math.e) / feats)
    hi, mid, lo = split3(sq)
    at = lax.broadcasted_iota(jnp.int32, (width - 3 * feats, count), 0)
    tail = jnp.where(at == 0, hi, jnp.where(at == 1, mid, jnp.where(at == 2, lo, 0.0)))
    tail = jnp.where((at >= 3) & (at < 6), 1.0, tail)
    return jnp.concatenate(parts + [tail.astype(BF16)], axis=0)


def kern(rows, cols):
    return jnp.exp2(dot(rows, cols)).astype(BF16)


def body(cfg, pts, cen, packed, out, kmat, colt, rowc, gath, reg, own_half, snd1, rcv1, snd2, rcv2,
         own_sum, fwd, csend, crecv, cown, full,
         as_, ar, fs, fr, b1s, b1r, b2s, b2r, gs, gr, hs, hr, cs, cr, ds_, dr):
    n_dp, n_c, feats, width = cfg
    n_h = n_c // 2
    d = lax.axis_index("dp")
    j = lax.axis_index("centers")
    par = lax.rem(j, 2)
    z = j // 2
    sib = j + 1 - 2 * par
    local_pts = pts.shape[0]
    local_cen = cen.shape[0]
    share = local_pts // n_c
    quarter = local_cen // n_dp
    step = min(512, local_cen)
    alpha_scale = 1.0 / math.sqrt(local_pts * n_dp)

    def up(t):
        return lax.rem(z + 1 + t, n_h)

    def down(t):
        return lax.rem(z + 2 * n_h - 1 - t, n_h)

    def dup(t):
        return lax.rem(d + 1 + t, n_dp)

    def ddown(t):
        return lax.rem(d + 2 * n_dp - 1 - t, n_dp)

    def copy(src, dst, ssem, rsem, dev):
        return pltpu.make_async_remote_copy(
            src_ref=src, dst_ref=dst, send_sem=ssem, recv_sem=rsem, device_id=dev, device_id_type=MESH
        )

    barrier = pltpu.get_barrier_semaphore()
    for t in range(n_h - 1):
        pl.semaphore_signal(barrier, inc=1, device_id=(d, 2 * up(t) + par), device_id_type=MESH)
    pl.semaphore_signal(barrier, inc=1, device_id=(d, sib), device_id_type=MESH)
    for t in range(n_dp - 1):
        pl.semaphore_signal(barrier, inc=1, device_id=(dup(t), j), device_id_type=MESH)

    for c in range(local_cen // step):
        at = pl.ds(c * step, step)
        colt[:, at] = col_form(packed[:feats, at], width)
        rowc[at, :] = row_form(cen[at, :], width)
    reg[...] = jnp.zeros_like(reg)

    pl.semaphore_wait(barrier, n_h - 1 + 1 + n_dp - 1)

    mine = packed.at[:, pl.ds(pl.multiple_of(d * quarter, 128), quarter)]

    def gather(t):
        return copy(mine, gath.at[j], as_.at[t], ar.at[t], (d, 2 * up(t) + par))

    def gather_in(t):
        return copy(mine, gath.at[2 * down(t) + par], as_.at[t], ar.at[t], (d, 2 * up(t) + par))

    for t in range(n_h - 1):
        gather(t).start()
    own_to_sib = copy(mine, gath.at[j], fs.at[n_h - 1], fr.at[n_h - 1], (d, sib))
    own_to_sib.start()
    gath[j] = packed[:, pl.ds(pl.multiple_of(d * quarter, 128), quarter)]

    def to_sib(t):
        return copy(snd1.at[t], rcv1.at[t], b1s.at[t], b1r.at[t], (d, sib))

    def to_peer(t):
        return copy(snd2.at[t], rcv2.at[t], b2s.at[t], b2r.at[t], (d, 2 * up(t) + par))

    def half(s):
        at = pl.ds(pl.multiple_of(s * share, share), share)
        rows = row_form(pts[at, :], width)
        acc = jnp.zeros((packed.shape[0] - feats, share), F32)
        for c in range(local_cen // step):
            cols = pl.ds(c * step, step)
            tile = kern(rows, colt[:, cols])
            kmat[at, cols] = tile
            acc = acc + dot_nt(packed[feats:, cols], tile)
        return acc

    @pl.loop(0, n_h)
    def _(t):
        zt = up(t)
        snd1[t] = half(2 * zt + 1 - par).astype(BF16)
        to_sib(t).start()
        own_half[...] = half(2 * zt + par)
        to_sib(t).wait_recv()
        total = own_half[...] + rcv1[t].astype(F32)

        @pl.when(t < n_h - 1)
        def _():
            snd2[t] = total.astype(BF16)
            to_peer(t).start()

        @pl.when(t == n_h - 1)
        def _():
            own_sum[...] = total

    def forward_block(t):
        at = gath.at[2 * down(t) + par]
        return copy(at, at, fs.at[t], fr.at[t], (d, sib))

    def forward_in(t):
        at = gath.at[2 * down(t) + 1 - par]
        return copy(at, at, fs.at[t], fr.at[t], (d, sib))

    for t in range(n_h - 1):
        gather_in(t).wait_recv()
        forward_block(t).start()

    def regular(block):
        cols = col_form(gath[block, :feats, :], width)
        weights = gath[block, feats:, :]
        for r in range(local_cen // step):
            rows = pl.ds(r * step, step)
            reg[:, rows] += dot_nt(weights, kern(rowc[rows, :], cols))

    @pl.loop(0, n_h)
    def _(i):
        regular(2 * i + par)

    for t in range(n_h - 1):
        to_peer(t).wait_recv()
    total = own_sum[...]
    for t in range(n_h - 1):
        total = total + rcv2[t].astype(F32)

    def slot(s):
        return fwd.at[:, pl.ds(pl.multiple_of(s * share, share), share)]

    def spread(t):
        return copy(slot(j), slot(j), gs.at[t], gr.at[t], (d, 2 * up(t) + par))

    def spread_in(t):
        at = slot(2 * down(t) + par)
        return copy(at, at, gs.at[t], gr.at[t], (d, 2 * up(t) + par))

    fwd[:, pl.ds(pl.multiple_of(j * share, share), share)] = total.astype(BF16)
    for t in range(n_h - 1):
        spread(t).start()
    own_fwd = copy(slot(j), slot(j), hs.at[n_h - 1], hr.at[n_h - 1], (d, sib))
    own_fwd.start()

    for t in range(n_h - 1):
        forward_in(t).wait_recv()
    own_sib_in = gath.at[sib]
    copy(own_sib_in, own_sib_in, fs.at[n_h - 1], fr.at[n_h - 1], (d, sib)).wait_recv()

    cut = (n_h * 3) // 4

    @pl.loop(0, cut)
    def _(i):
        regular(2 * i + 1 - par)

    def relay(t):
        at = slot(2 * down(t) + par)
        return copy(at, at, hs.at[t], hr.at[t], (d, sib))

    def relay_in(t):
        at = slot(2 * down(t) + 1 - par)
        return copy(at, at, hs.at[t], hr.at[t], (d, sib))

    for t in range(n_h - 1):
        spread_in(t).wait_recv()
        relay(t).start()

    @pl.loop(cut, n_h)
    def _(i):
        regular(2 * i + 1 - par)

    for t in range(n_h - 1):
        relay_in(t).wait_recv()
    copy(slot(sib), slot(sib), hs.at[n_h - 1], hr.at[n_h - 1], (d, sib)).wait_recv()

    def cross(t):
        return copy(csend.at[t], crecv.at[t], cs.at[t], cr.at[t], (dup(t), j))

    @pl.loop(0, n_dp)
    def _(t):
        at = pl.ds(pl.multiple_of(dup(t) * quarter, 128), quarter)
        back = dot(fwd[...], kmat[:, at]) * alpha_scale + reg[:, at]

        @pl.when(t < n_dp - 1)
        def _():
            csend[t] = back
            cross(t).start()

        @pl.when(t == n_dp - 1)
        def _():
            cown[...] = back

    for t in range(n_dp - 1):
        cross(t).wait_recv()
    total = cown[...]
    for t in range(n_dp - 1):
        total = total + crecv[t]
    full[d] = total

    def publish(t):
        return copy(full.at[d], full.at[d], ds_.at[t], dr.at[t], (dup(t), j))

    def publish_in(t):
        at = full.at[ddown(t)]
        return copy(at, at, ds_.at[t], dr.at[t], (dup(t), j))

    for t in range(n_dp - 1):
        publish(t).start()
    for t in range(n_h - 1):
        gather(t).wait_send()
        forward_block(t).wait_send()
        to_peer(t).wait_send()
        spread(t).wait_send()
        relay(t).wait_send()
    for t in range(n_h):
        to_sib(t).wait_send()
    own_to_sib.wait_send()
    own_fwd.wait_send()
    for t in range(n_dp - 1):
        cross(t).wait_send()
    for t in range(n_dp - 1):
        publish_in(t).wait_recv()
    for t in range(n_dp - 1):
        publish(t).wait_send()
    for q in range(n_dp):
        out[:, q * quarter:(q + 1) * quarter] = full[q]


def solution(mesh):
    n_dp, n_c = mesh.shape["dp"], mesh.shape["centers"]

    def on_device(points, centers, coef):
        local_pts, feats = points.shape
        local_cen, outs = coef.shape
        width = -(-(3 * feats + 6) // 128) * 128
        n_h = n_c // 2
        share, quarter = local_pts // n_c, local_cen // n_dp
        packed = jnp.concatenate([centers, coef], axis=1).T
        dma = pltpu.SemaphoreType.DMA
        result = pl.pallas_call(
            functools.partial(body, (n_dp, n_c, feats, width)),
            out_shape=jax.ShapeDtypeStruct((outs, local_cen), F32),
            in_specs=[pl.BlockSpec(memory_space=pltpu.VMEM)] * 3,
            out_specs=pl.BlockSpec(memory_space=pltpu.VMEM),
            scratch_shapes=[
                pltpu.VMEM((local_pts, local_cen), BF16),
                pltpu.VMEM((width, local_cen), BF16),
                pltpu.VMEM((local_cen, width), BF16),
                pltpu.VMEM((n_c, feats + outs, quarter), BF16),
                pltpu.VMEM((outs, local_cen), F32),
                pltpu.VMEM((outs, share), F32),
                pltpu.VMEM((n_h, outs, share), BF16),
                pltpu.VMEM((n_h, outs, share), BF16),
                pltpu.VMEM((n_h, outs, share), BF16),
                pltpu.VMEM((n_h, outs, share), BF16),
                pltpu.VMEM((outs, share), F32),
                pltpu.VMEM((outs, local_pts), BF16),
                pltpu.VMEM((n_dp, outs, quarter), F32),
                pltpu.VMEM((n_dp, outs, quarter), F32),
                pltpu.VMEM((outs, quarter), F32),
                pltpu.VMEM((n_dp, outs, quarter), F32),
            ] + [dma((n_h,))] * 12 + [dma((n_dp,))] * 4,
            compiler_params=pltpu.CompilerParams(
                collective_id=0, has_side_effects=True, vmem_limit_bytes=60 * 1024 * 1024
            ),
        )(points, centers, packed)
        return result.T

    return jax.shard_map(
        on_device,
        mesh=mesh,
        in_specs=(P("dp", None), P("centers", None), P("centers", None)),
        out_specs=P("centers", None),
        check_vma=False,
    )
```

time: 193 us -> 56.4 us (0.29)
  waiting for transfers between devices: 105 us -> 0 us
  Pallas kernels: 0 us -> 50.2 us
  matrix products: 49 us -> 0 us
  blocking collectives: 16.8 us -> 0 us
  between operations: 13.2 us -> 0.01 us
  other arithmetic: 4.13 us -> 1.79 us
    pallas_call x0 -> x1, Pallas kernels: none -> 50.2 us  [on_device(): pl.pallas_call(functools.partial(body, (n_dp, n_c, feats, width)), out_sh...]
    dot_general x10 -> x0, matrix products: 49 us -> none  [the longest x4 17.6 us: kernel_block(): lax.dot_general(left_pts, right_pts, (((1,), (1,)), ((), ())), preferred_...]
    psum x1 -> x0, waiting for transfers between devices: 44.9 us -> none  [on_device(): return lax.psum(back + placed, 'dp')]
    reduce_scatter x1 -> x0, waiting for transfers between devices: 31.9 us -> none  [on_device(): lax.psum_scatter(forward_part.astype(jnp.bfloat16), 'centers', scatter_di...]
    all_gather x2 -> x0, waiting for transfers between devices: 26.5 us -> none  [the longest x1 26.4 us: on_device(): piece_coef = lax.all_gather(coef, 'centers', axis=0, tiled=True)]
    all_gather x1 -> x0, blocking collectives: 16.8 us -> none  [on_device(): forward = lax.all_gather(shared, 'centers', axis=0, tiled=True)]
    reduce_sum x7 -> x0, other arithmetic: 4.13 us -> none  [squares(): return jnp.sum(wide * wide, axis=1)]
    unnamed x4 -> x7, local copies, waits for them, and re-layouts: 4.08 us -> 4.2 us
  transfers between devices with their start and end apart: 4 -> 0, of which waited for: 3 -> 0; matrix products, arithmetic and copies ran while one was open for 6% -> 0% of each run, Pallas kernels for 0% -> 0%
where the time goes in v1:
time: 56.4 us; the launch traced here: 56.2 us
  Pallas kernels  50.2 us (89%)
  local copies, waits for them, and re-layouts  4.2 us (7%)
  other arithmetic  1.79 us (3%)
    pallas_call x1, Pallas kernels, on_device(): pl.pallas_call(functools.partial(body, (n_dp, n_c, feats, width)), out_sh...  50.2 us
    unnamed x7, local copies, waits for them, and re-layouts  4.2 us
    transpose x1, other arithmetic, on_device(): packed = jnp.concatenate([centers, coef], axis=1).T  1.79 us

profile of v1, /device:TPU:0, one launch (start us, length us, event | category | flops | bytes accessed | tf_op | source)
XLA Modules:
  0.0 56.2 jit_solution(1340230132601358517)
XLA Ops:
  0.0 0.0 copy-start
  0.0 1.8 %maximum_bitcast_fusion.packed = bf16[96,2048]{1,0:T(8,128)(2,1)} fusion(bf16[2048,64]{0,1:T(8,128)(2,1)} %param.5, bf16[2048,32]{0,1:T(8,128)(2,1)} %param.4), kind=kLoop, calls=%fused_computation | loop fusion | flops 786432 | bytes 786432 | tf_op jit(solution)/shard_map/transpose | solution.py:296
  1.8 0.0 copy-done
  1.8 0.0 copy-start.1
  1.8 1.0 %copy.5.cen = bf16[2048,32]{1,0:T(8,128)(2,1)} copy(bf16[2048,32]{0,1:T(8,128)(2,1)S(1)} %copy-done) | data formatting | bytes 262144 | tf_op args[1]
  2.8 0.0 copy-done.1
  2.8 1.3 %copy.4.pts = bf16[4096,32]{1,0:T(8,128)(2,1)} copy(bf16[4096,32]{0,1:T(8,128)(2,1)S(1)} %copy-done.1) | data formatting | bytes 524288 | tf_op args[0]
  4.1 50.2 %shard_map.37 = f32[64,2048]{1,0:T(8,128)} custom-call(bf16[4096,32]{1,0:T(8,128)(2,1)} %copy.4.pts, bf16[2048,32]{1,0:T(8,128)(2,1)} %copy.5.cen, bf16[96,2048]{1,0:T(8,128)(2,1)} %maximum_bitcast_fusion.packed), custom_call_target="tpu_custom_call" | custom-call | tf_op jit(solution)/shard_map/pallas_call | solution.py:298
  54.3 1.9 %copy.7 = f32[2048,64]{0,1:T(8,128)} copy(f32[2048,64]{0,1:T(8,128)} %bitcast.3) | data formatting | bytes 1048576
Async XLA Ops:
  0.0 1.8 %copy-start = (bf16[2048,32]{0,1:T(8,128)(2,1)S(1)}, bf16[2048,32]{0,1:T(8,128)(2,1)}, u32[]{:S(2)}) copy-start(bf16[2048,32]{0,1:T(8,128)(2,1)} %param.4) | copy-start | bytes 393220
  1.8 1.0 %copy-start.1 = (bf16[4096,32]{0,1:T(8,128)(2,1)S(1)}, bf16[4096,32]{0,1:T(8,128)(2,1)}, u32[]{:S(2)}) copy-start(bf16[4096,32]{0,1:T(8,128)(2,1)} %param.3) | copy-start | bytes 786436

commit v2 on v1

--- a/solution.py
+++ b/solution.py
@@ -57,7 +57,7 @@
     return jnp.exp2(dot(rows, cols)).astype(BF16)
 
 
-def body(cfg, pts, cen, packed, out, kmat, colt, rowc, gath, reg, own_half, snd1, rcv1, snd2, rcv2,
+def body(cfg, pts_hbm, cen_hbm, packed, out, pts, cen, lsem, sibp, kmat, colt, rowc, gath, reg, own_half, snd1, rcv1, snd2, rcv2,
          own_sum, fwd, csend, crecv, cown, full,
          as_, ar, fs, fr, b1s, b1r, b2s, b2r, gs, gr, hs, hr, cs, cr, ds_, dr):
     n_dp, n_c, feats, width = cfg
@@ -71,7 +71,7 @@
     local_cen = cen.shape[0]
     share = local_pts // n_c
     quarter = local_cen // n_dp
-    step = min(512, local_cen)
+    step = min(1024, local_cen)
     alpha_scale = 1.0 / math.sqrt(local_pts * n_dp)
 
     def up(t):
@@ -98,9 +98,16 @@
     for t in range(n_dp - 1):
         pl.semaphore_signal(barrier, inc=1, device_id=(dup(t), j), device_id_type=MESH)
 
+    cen_in = pltpu.make_async_copy(cen_hbm, cen, lsem.at[0])
+    pts_in = pltpu.make_async_copy(pts_hbm, pts, lsem.at[1])
+    cen_in.start()
+    pts_in.start()
     for c in range(local_cen // step):
         at = pl.ds(c * step, step)
         colt[:, at] = col_form(packed[:feats, at], width)
+    cen_in.wait()
+    for c in range(local_cen // step):
+        at = pl.ds(c * step, step)
         rowc[at, :] = row_form(cen[at, :], width)
     reg[...] = jnp.zeros_like(reg)
 
@@ -116,9 +123,9 @@
 
     for t in range(n_h - 1):
         gather(t).start()
-    own_to_sib = copy(mine, gath.at[j], fs.at[n_h - 1], fr.at[n_h - 1], (d, sib))
+    own_to_sib = copy(packed, sibp, fs.at[n_h - 1], fr.at[n_h - 1], (d, sib))
     own_to_sib.start()
-    gath[j] = packed[:, pl.ds(pl.multiple_of(d * quarter, 128), quarter)]
+    pts_in.wait()
 
     def to_sib(t):
         return copy(snd1.at[t], rcv1.at[t], b1s.at[t], b1r.at[t], (d, sib))
@@ -174,10 +181,6 @@
             rows = pl.ds(r * step, step)
             reg[:, rows] += dot_nt(weights, kern(rowc[rows, :], cols))
 
-    @pl.loop(0, n_h)
-    def _(i):
-        regular(2 * i + par)
-
     for t in range(n_h - 1):
         to_peer(t).wait_recv()
     total = own_sum[...]
@@ -200,16 +203,18 @@
     own_fwd = copy(slot(j), slot(j), hs.at[n_h - 1], hr.at[n_h - 1], (d, sib))
     own_fwd.start()
 
+    @pl.loop(0, n_h - 1)
+    def _(i):
+        regular(2 * up(i) + par)
+
     for t in range(n_h - 1):
         forward_in(t).wait_recv()
-    own_sib_in = gath.at[sib]
-    copy(own_sib_in, own_sib_in, fs.at[n_h - 1], fr.at[n_h - 1], (d, sib)).wait_recv()
-
-    cut = (n_h * 3) // 4
+
+    cut = ((n_h - 1) * 2) // 3
 
     @pl.loop(0, cut)
     def _(i):
-        regular(2 * i + 1 - par)
+        regular(2 * up(i) + 1 - par)
 
     def relay(t):
         at = slot(2 * down(t) + par)
@@ -223,9 +228,9 @@
         spread_in(t).wait_recv()
         relay(t).start()
 
-    @pl.loop(cut, n_h)
+    @pl.loop(cut, n_h - 1)
     def _(i):
-        regular(2 * i + 1 - par)
+        regular(2 * up(i) + 1 - par)
 
     for t in range(n_h - 1):
         relay_in(t).wait_recv()
@@ -247,6 +252,13 @@
         @pl.when(t == n_dp - 1)
         def _():
             cown[...] = back
+
+    own_to_sib.wait_recv()
+    mine_rows = rowc[pl.ds(pl.multiple_of(d * quarter, 128), quarter), :]
+    for c in range(local_cen // step):
+        at = pl.ds(c * step, step)
+        cown[...] += dot_nt(packed[feats:, at], kern(mine_rows, colt[:, at]))
+        cown[...] += dot_nt(sibp[feats:, at], kern(mine_rows, col_form(sibp[:feats, at], width)))
 
     for t in range(n_dp - 1):
         cross(t).wait_recv()
@@ -298,9 +310,13 @@
         result = pl.pallas_call(
             functools.partial(body, (n_dp, n_c, feats, width)),
             out_shape=jax.ShapeDtypeStruct((outs, local_cen), F32),
-            in_specs=[pl.BlockSpec(memory_space=pltpu.VMEM)] * 3,
+            in_specs=[pl.BlockSpec(memory_space=pl.ANY)] * 2 + [pl.BlockSpec(memory_space=pltpu.VMEM)],
             out_specs=pl.BlockSpec(memory_space=pltpu.VMEM),
             scratch_shapes=[
+                pltpu.VMEM((local_pts, feats), BF16),
+                pltpu.VMEM((local_cen, feats), BF16),
+                dma((2,)),
+                pltpu.VMEM((feats + outs, local_cen), BF16),
                 pltpu.VMEM((local_pts, local_cen), BF16),
                 pltpu.VMEM((width, local_cen), BF16),
                 pltpu.VMEM((local_cen, width), BF16),

time: 56.4 us -> 53.6 us (0.950)
  Pallas kernels: 50.2 us -> 47.3 us
    pallas_call x1, Pallas kernels: 50.2 us -> 47.3 us  [on_device(): pl.pallas_call(functools.partial(body, (n_dp, n_c, feats, width)), out_sh...]
where the time goes in v2:
time: 53.6 us; the launch traced here: 53.3 us
  Pallas kernels  47.3 us (88%)
  local copies, waits for them, and re-layouts  4.2 us (8%)
  other arithmetic  1.79 us (3%)
    pallas_call x1, Pallas kernels, on_device(): pl.pallas_call(functools.partial(body, (n_dp, n_c, feats, width)), out_sh...  47.3 us
    unnamed x7, local copies, waits for them, and re-layouts  4.2 us
    transpose x1, other arithmetic, on_device(): packed = jnp.concatenate([centers, coef], axis=1).T  1.79 us

profile of v2, /device:TPU:0, one launch (start us, length us, event | category | flops | bytes accessed | tf_op | source)
XLA Modules:
  0.0 53.3 jit_solution(6235959549221851688)
XLA Ops:
  0.0 0.0 copy-start
  0.0 1.8 %maximum_bitcast_fusion.packed = bf16[96,2048]{1,0:T(8,128)(2,1)} fusion(bf16[2048,64]{0,1:T(8,128)(2,1)} %param.5, bf16[2048,32]{0,1:T(8,128)(2,1)} %param.4), kind=kLoop, calls=%fused_computation | loop fusion | flops 786432 | bytes 786432 | tf_op jit(solution)/shard_map/transpose | solution.py:308
  1.8 0.0 copy-done
  1.8 0.0 copy-start.1
  1.8 1.0 %copy.5.cen_hbm = bf16[2048,32]{1,0:T(8,128)(2,1)} copy(bf16[2048,32]{0,1:T(8,128)(2,1)S(1)} %copy-done) | data formatting | bytes 262144 | tf_op args[1]
  2.8 0.0 copy-done.1
  2.8 1.3 %copy.4.pts_hbm = bf16[4096,32]{1,0:T(8,128)(2,1)} copy(bf16[4096,32]{0,1:T(8,128)(2,1)S(1)} %copy-done.1) | data formatting | bytes 524288 | tf_op args[0]
  4.1 47.3 %shard_map.37 = f32[64,2048]{1,0:T(8,128)} custom-call(bf16[4096,32]{1,0:T(8,128)(2,1)} %copy.4.pts_hbm, bf16[2048,32]{1,0:T(8,128)(2,1)} %copy.5.cen_hbm, bf16[96,2048]{1,0:T(8,128)(2,1)} %maximum_bitcast_fusion.packed), custom_call_target="tpu_custom_call" | custom-call | tf_op jit(solution)/shard_map/pallas_call | solution.py:310
  51.4 1.9 %copy.7 = f32[2048,64]{0,1:T(8,128)} copy(f32[2048,64]{0,1:T(8,128)} %bitcast.3) | data formatting | bytes 1048576
Async XLA Ops:
  0.0 1.8 %copy-start = (bf16[2048,32]{0,1:T(8,128)(2,1)S(1)}, bf16[2048,32]{0,1:T(8,128)(2,1)}, u32[]{:S(2)}) copy-start(bf16[2048,32]{0,1:T(8,128)(2,1)} %param.4) | copy-start | bytes 393220
  1.8 1.0 %copy-start.1 = (bf16[4096,32]{0,1:T(8,128)(2,1)S(1)}, bf16[4096,32]{0,1:T(8,128)(2,1)}, u32[]{:S(2)}) copy-start(bf16[4096,32]{0,1:T(8,128)(2,1)} %param.3) | copy-start | bytes 786436
